TPU v7x, 8 devices: a whole 2x2x1 slice. The times are simulated.
8 devices in a mesh: dp: 1 (over z), tp: 2 (over y), cp: 4 (over x, core).
Axes of the slice: x: 2, y: 2, z: 1, core: 2. Of those that a mesh axis runs over, the one named last changes fastest.
Arguments:
- x_in: bfloat16 [4096, 4096], P(('dp', 'cp'))
- positions: int32 [4096], P(('dp', 'cp'))
- norm_gain: bfloat16 [4096], replicated
- w_q: bfloat16 [4096, 4096], P(None, 'tp')
- w_k: bfloat16 [4096, 1024], P(None, 'tp')
- w_v: bfloat16 [4096, 1024], P(None, 'tp')
- w_o: bfloat16 [4096, 4096], P('tp')
Outputs:
- output 1: bfloat16 [4096, 4096], P(('dp', 'cp'))
- output 2: bfloat16 [4096, 8, 128], P(('dp', 'cp'), 'tp')
- output 3: bfloat16 [4096, 8, 128], P(('dp', 'cp'), 'tp')
All inputs are finite; a program needn't handle non-finite values.
Results may differ from a plain program's by a relative error of at most 0.00960483.
Values are sent between devices in bfloat16 or wider.
A program may use at most 1 GiB of HBM per device.

v0:
```python
import math
import jax
import jax.numpy as jnp
from jax import lax
from jax.sharding import PartitionSpec as P

HEAD_DIM = 128
NORM_EPS = 1e-5


def rope_freqs():
    exponent = jnp.arange(0, HEAD_DIM, 2).astype(jnp.float32) / HEAD_DIM
    base_freq = 1.0 / (500000.0 ** exponent)
    wave_len = 2.0 * math.pi / base_freq
    smooth = (8192.0 / wave_len - 1.0) / 3.0
    blended = (1.0 - smooth) * base_freq / 8.0 + smooth * base_freq
    return jnp.where(wave_len < 2048.0, base_freq, jnp.where(wave_len > 8192.0, base_freq / 8.0, blended))


def apply_rope(vecs, positions, freqs):
    half_dim = HEAD_DIM // 2
    angles = positions.astype(jnp.float32)[:, None] * freqs[None, :]
    cosine = jnp.cos(angles)[:, None, :]
    sine_val = jnp.sin(angles)[:, None, :]
    vec_f32 = vecs.astype(jnp.float32)
    first_half = vec_f32[..., :half_dim]
    second_half = vec_f32[..., half_dim:]
    return jnp.concatenate([first_half * cosine - second_half * sine_val, second_half * cosine + first_half * sine_val], axis=-1).astype(jnp.bfloat16)


def rms_norm(x_rows, norm_gain):
    x_f32 = x_rows.astype(jnp.float32)
    normed = x_f32 * lax.rsqrt(jnp.mean(x_f32 * x_f32, axis=-1, keepdims=True) + NORM_EPS)
    return (normed * norm_gain.astype(jnp.float32)[None, :]).astype(jnp.bfloat16)


def query_block(q_rows, key_rows, heads):
    blk_rows = q_rows
    while blk_rows % 2 == 0 and blk_rows > 8 and blk_rows * key_rows * heads > 2 ** 24:
        blk_rows = blk_rows // 2
    return blk_rows


def attend_all(queries, q_pos, keys, values, key_pos):
    q_rows = queries.shape[0]
    kv_heads = queries.shape[1]
    group_size = queries.shape[2]
    blk_rows = query_block(q_rows, keys.shape[0], kv_heads * group_size)
    n_blocks = q_rows // blk_rows
    q_blocks = queries.reshape(n_blocks, blk_rows, kv_heads, group_size, HEAD_DIM)
    pos_blocks = q_pos.reshape(n_blocks, blk_rows)
    score_scale = 1.0 / math.sqrt(HEAD_DIM)

    def one_block(block):
        q_part, pos_part = block
        scores = jnp.einsum('qhgd,thd->qhgt', q_part, keys, preferred_element_type=jnp.float32) * score_scale
        keep_mask = key_pos[None, None, None, :] <= pos_part[:, None, None, None]
        scores = jnp.where(keep_mask, scores, -jnp.inf)
        prob_bf = jax.nn.softmax(scores, axis=-1).astype(jnp.bfloat16)
        return jnp.einsum('qhgt,thd->qhgd', prob_bf, values, preferred_element_type=jnp.float32).astype(jnp.bfloat16)

    o_blocks = lax.map(one_block, (q_blocks, pos_blocks))
    return o_blocks.reshape(q_rows, kv_heads * group_size * HEAD_DIM)


def solution(mesh):
    n_tp = mesh.shape['tp']

    def device_fn(x_in, positions, norm_gain, w_q, w_k, w_v, w_o):
        local_rows = x_in.shape[0]
        heads_dev = w_q.shape[1] // HEAD_DIM
        kv_dev = w_k.shape[1] // HEAD_DIM
        group_size = heads_dev // kv_dev
        hidden = rms_norm(x_in, norm_gain)
        freqs = rope_freqs()
        queries = jnp.dot(hidden, w_q, preferred_element_type=jnp.float32).astype(jnp.bfloat16).reshape(local_rows, heads_dev, HEAD_DIM)
        keys = jnp.dot(hidden, w_k, preferred_element_type=jnp.float32).astype(jnp.bfloat16).reshape(local_rows, kv_dev, HEAD_DIM)
        values = jnp.dot(hidden, w_v, preferred_element_type=jnp.float32).astype(jnp.bfloat16).reshape(local_rows, kv_dev, HEAD_DIM)
        queries = apply_rope(queries, positions, freqs).reshape(local_rows, kv_dev, group_size, HEAD_DIM)
        keys = apply_rope(keys, positions, freqs)
        keys_all = lax.all_gather(keys, 'cp', axis=0, tiled=True)
        values_all = lax.all_gather(values, 'cp', axis=0, tiled=True)
        pos_all = lax.all_gather(positions, 'cp', axis=0, tiled=True)
        attn = attend_all(queries, positions, keys_all, values_all, pos_all)
        part_out = jnp.dot(attn, w_o, preferred_element_type=jnp.float32)
        summed = lax.psum_scatter(part_out, 'tp', scatter_dimension=0, tiled=True)
        share_rows = local_rows // n_tp
        x_share = lax.dynamic_slice_in_dim(x_in, lax.axis_index('tp') * share_rows, share_rows, axis=0)
        y_share = (x_share.astype(jnp.float32) + summed).astype(jnp.bfloat16)
        y_out = lax.all_gather(y_share, 'tp', axis=0, tiled=True)
        return y_out, keys, values

    row_spec = P(('dp', 'cp'), None)
    cache_spec = P(('dp', 'cp'), 'tp', None)
    return jax.shard_map(device_fn, mesh=mesh, in_specs=(row_spec, P(('dp', 'cp')), P(None), P(None, 'tp'), P(None, 'tp'), P(None, 'tp'), P('tp', None)), out_specs=(row_spec, cache_spec, cache_spec), check_vma=False)
```

profile of v0, /device:TPU:0, one launch (start us, length us, event | category | flops | bytes accessed | tf_op | source)
XLA Modules:
  0.0 693.3 jit_solution(16870999611882805514)
XLA Ops:
  7.2 0.0 all-gather.4.cloned.1.call-start
  7.2 0.7 convert_element_type.61
  7.9 0.0 copy-start
  7.9 5.2 fusion.39
  13.2 0.5 copy-done
  13.7 6.9 convolution_convert_fusion.1
  20.6 1.2 fusion.54
  21.8 0.0 copy-start.3
  21.8 1.9 copy.53
  23.7 1.7 copy.54
  25.4 0.0 copy-done.3
  25.4 1.0 multiply_cosine_fusion
  26.4 0.2 copy.40
  26.6 1.0 copy.42
  27.6 2.4 subtract_convert_fusion.1
  30.0 2.4 pad_maximum_fusion.1
  32.4 0.0 all-gather.4.cloned.1.call-update
  32.4 0.2 all-gather.6.cloned.1.call-start
  32.7 9.2 %convolution_convert_fusion = bf16[1024,512]{0,1:T(8,128)(2,1)S(1)} fusion(bf16[4096,512]{1,0:T(8,128)(2,1)} %param.14, bf16[1024,4096]{1,0:T(8,128)(2,1)} %param.9, f32[4096]{0:T(1024)S(1)} %convert_element_type.61, f32[1024]{0:T(1024)S(1)} %add_rsqrt_fusion), kind=kOutput, calls=%fused_computation.41 | convolution fusion | flops 4312268800 | bytes 13651968 | tf_op jit(solution)/shard_map/dot_general | solution.py:78
  41.9 0.0 copy-start.1
  41.9 1.3 copy.43
  43.2 0.0 all-gather.6.cloned.1.call-update
  43.3 0.0 reduce-scatter.2.cloned.1.call-start
  43.3 24.2 %convert_convert_fusion = f32[1024,2048]{1,0:T(8,128)} fusion(bf16[4096,2048]{1,0:T(8,128)(2,1)} %param.12, bf16[1024,4096]{1,0:T(8,128)(2,1)} %param.9, f32[4096]{0:T(1024)S(1)} %convert_element_type.61, f32[1024]{0:T(1024)S(1)} %add_rsqrt_fusion), kind=kOutput, calls=%fused_computation.38 | convolution fusion | flops 17200840704 | bytes 33574912 | tf_op jit(solution)/shard_map/dot_general | solution.py:76
  67.5 0.0 copy-done.1
  67.5 9.3 %copy.50 = f32[1024,2048]{0,1:T(8,128)} copy(f32[1024,2048]{1,0:T(8,128)} %convert_convert_fusion) | data formatting | bytes 16777216 | tf_op jit(solution)/shard_map/convert_element_type | solution.py:25
  76.8 6.2 subtract_convert_fusion
  83.0 4.6 concatenate.13
  87.6 2.7 concatenate.14
  90.3 6.9 %pad_maximum_fusion = bf16[4,256,4,4,128]{1,0,4,3,2:T(4,128)(2,1)} fusion(bf16[4,256,4,4,64]{1,0,4,3,2:T(4,128)(2,1)} %concatenate.14, bf16[4,256,4,4,64]{1,0,4,3,2:T(4,128)(2,1)} %concatenate.13), kind=kLoop, calls=%fused_computation.35 | loop fusion | flops 2097152 | bytes 8388608 | tf_op jit(solution)/shard_map/concatenate | solution.py:28
  97.2 7.5 %copy.44 = bf16[4,256,4,4,128]{4,1,3,2,0:T(8,128)(2,1)} copy(bf16[4,256,4,4,128]{1,0,4,3,2:T(4,128)(2,1)} %pad_maximum_fusion) | data formatting | bytes 8388608 | tf_op jit(solution)/shard_map/while | solution.py:62
  104.8 10.2 %all_gather.12 = s32[4096]{0:T(1024)S(1)} all-gather(s32[1024]{0:T(1024)S(1)} %copy-done.3), channel_id=1, replica_groups=mesh['dp'=1,'tp'=2,'cp'=4] {'cp'}, dimensions={0}, use_global_device_ids=true | all-gather | bytes 20480 | tf_op jit(solution)/shard_map/all_gather | solution.py:83
  115.0 0.0 all-gather.4.cloned.1.call-done
  115.0 4.7 copy.45
  119.7 0.0 all-gather.6.cloned.1.call-done
  119.7 230.1 %while.10 = (s32[]{:T(128)}, bf16[4,256,4,4,128]{4,3,2,1,0:T(4,128)(2,1)}, s32[4096]{0:T(1024)S(1)}, s32[4,256]{1,0:T(4,128)S(1)}, bf16[4,256,4,4,128]{4,1,3,2,0...) while((s32[]{:T(128)}, ...), condition=%wide.region_4.5_spmd, body=%wide.region_1.4_spmd.sunk | while | flops 8692174848 | bytes 148951136 | solution.py:62
  119.7 0.6 broadcast_compare_fusion.2
  120.4 31.1 %fusion.69 = (f32[256,4,4]{0,2,1:T(4,128)S(1)}, f32[256,4,4,4096]{3,0,2,1:T(8,128)}) fusion(pred[256,4096]{1,0:T(8,128)(4,1)S(1)} %broadcast_compare_fusion.2, bf16[4096,4,128]{2,0,1:T(8,128)(2,1)} %get-tuple-element.173, bf16[4,256,4,4,128]{4,1,3,2,0:T(8,128)(2,1)} %get-tuple-element.172, s32[]{:T(128)} %get-tuple-element.160), kind=kOutput, calls=%fused_computation.49.clone.1 | convolution fusion | flops 4362080256 | bytes 73417216 | tf_op jit(solution)/shard_map/while/body/eval_jaxpr/sub | solution.py:59
  151.4 24.0 %fusion.70 = bf16[1,256,4,4,128]{4,1,3,2,0:T(8,128)(2,1)S(1)} fusion(bf16[4096,4,128]{2,0,1:T(8,128)(2,1)} %get-tuple-element.174, f32[256,4,4,4096]{3,0,2,1:T(8,128)} %get-tuple-element.150, f32[256,4,4]{0,2,1:T(4,128)S(1)} %get-tuple-element.151), kind=kOutput, calls=%fused_computation.18.clone.1 | convolution fusion | flops 4329046016 | bytes 72368128 | tf_op jit(solution)/shard_map/while/body/eval_jaxpr/qhgt,thd->qhgd/dot_general | solution.py:60
  175.4 1.9 copy_dynamic-update-slice_fusion.2
  177.3 0.6 broadcast_compare_fusion.2
  177.9 31.1 %fusion.69 = (f32[256,4,4]{0,2,1:T(4,128)S(1)}, f32[256,4,4,4096]{3,0,2,1:T(8,128)}) fusion(pred[256,4096]{1,0:T(8,128)(4,1)S(1)} %broadcast_compare_fusion.2, bf16[4096,4,128]{2,0,1:T(8,128)(2,1)} %get-tuple-element.173, bf16[4,256,4,4,128]{4,1,3,2,0:T(8,128)(2,1)} %get-tuple-element.172, s32[]{:T(128)} %get-tuple-element.160), kind=kOutput, calls=%fused_computation.49.clone.1 | convolution fusion | flops 4362080256 | bytes 73417216 | tf_op jit(solution)/shard_map/while/body/eval_jaxpr/sub | solution.py:59
  209.0 24.0 %fusion.70 = bf16[1,256,4,4,128]{4,1,3,2,0:T(8,128)(2,1)S(1)} fusion(bf16[4096,4,128]{2,0,1:T(8,128)(2,1)} %get-tuple-element.174, f32[256,4,4,4096]{3,0,2,1:T(8,128)} %get-tuple-element.150, f32[256,4,4]{0,2,1:T(4,128)S(1)} %get-tuple-element.151), kind=kOutput, calls=%fused_computation.18.clone.1 | convolution fusion | flops 4329046016 | bytes 72368128 | tf_op jit(solution)/shard_map/while/body/eval_jaxpr/qhgt,thd->qhgd/dot_general | solution.py:60
  233.0 1.8 copy_dynamic-update-slice_fusion.2
  234.8 0.6 broadcast_compare_fusion.2
  235.4 31.1 %fusion.69 = (f32[256,4,4]{0,2,1:T(4,128)S(1)}, f32[256,4,4,4096]{3,0,2,1:T(8,128)}) fusion(pred[256,4096]{1,0:T(8,128)(4,1)S(1)} %broadcast_compare_fusion.2, bf16[4096,4,128]{2,0,1:T(8,128)(2,1)} %get-tuple-element.173, bf16[4,256,4,4,128]{4,1,3,2,0:T(8,128)(2,1)} %get-tuple-element.172, s32[]{:T(128)} %get-tuple-element.160), kind=kOutput, calls=%fused_computation.49.clone.1 | convolution fusion | flops 4362080256 | bytes 73417216 | tf_op jit(solution)/shard_map/while/body/eval_jaxpr/sub | solution.py:59
  266.5 24.0 %fusion.70 = bf16[1,256,4,4,128]{4,1,3,2,0:T(8,128)(2,1)S(1)} fusion(bf16[4096,4,128]{2,0,1:T(8,128)(2,1)} %get-tuple-element.174, f32[256,4,4,4096]{3,0,2,1:T(8,128)} %get-tuple-element.150, f32[256,4,4]{0,2,1:T(4,128)S(1)} %get-tuple-element.151), kind=kOutput, calls=%fused_computation.18.clone.1 | convolution fusion | flops 4329046016 | bytes 72368128 | tf_op jit(solution)/shard_map/while/body/eval_jaxpr/qhgt,thd->qhgd/dot_general | solution.py:60
  290.5 1.8 copy_dynamic-update-slice_fusion.2
  292.3 0.6 broadcast_compare_fusion.2
  292.9 31.1 %fusion.69 = (f32[256,4,4]{0,2,1:T(4,128)S(1)}, f32[256,4,4,4096]{3,0,2,1:T(8,128)}) fusion(pred[256,4096]{1,0:T(8,128)(4,1)S(1)} %broadcast_compare_fusion.2, bf16[4096,4,128]{2,0,1:T(8,128)(2,1)} %get-tuple-element.173, bf16[4,256,4,4,128]{4,1,3,2,0:T(8,128)(2,1)} %get-tuple-element.172, s32[]{:T(128)} %get-tuple-element.160), kind=kOutput, calls=%fused_computation.49.clone.1 | convolution fusion | flops 4362080256 | bytes 73417216 | tf_op jit(solution)/shard_map/while/body/eval_jaxpr/sub | solution.py:59
  324.0 24.0 %fusion.70 = bf16[1,256,4,4,128]{4,1,3,2,0:T(8,128)(2,1)S(1)} fusion(bf16[4096,4,128]{2,0,1:T(8,128)(2,1)} %get-tuple-element.174, f32[256,4,4,4096]{3,0,2,1:T(8,128)} %get-tuple-element.150, f32[256,4,4]{0,2,1:T(4,128)S(1)} %get-tuple-element.151), kind=kOutput, calls=%fused_computation.18.clone.1 | convolution fusion | flops 4329046016 | bytes 72368128 | tf_op jit(solution)/shard_map/while/body/eval_jaxpr/qhgt,thd->qhgd/dot_general | solution.py:60
  348.0 1.9 copy_dynamic-update-slice_fusion.2
  349.9 7.8 %reshape.139 = bf16[1024,2048]{1,0:T(8,128)(2,1)} reshape(bf16[4,256,4,4,128]{4,3,2,1,0:T(4,128)(2,1)} %get-tuple-element.40) | data formatting | bytes 8388608 | tf_op jit(solution)/shard_map/reshape | solution.py:63
  357.6 23.7 %fusion.55 = f32[1024,4096]{1,0:T(8,128)} fusion(bf16[1024,2048]{1,0:T(8,128)(2,1)} %reshape.139, bf16[2048,4096]{1,0:T(8,128)(2,1)} %param.15), kind=kOutput, calls=%fused_computation.51 | convolution fusion | flops 17179869184 | bytes 37748736 | tf_op jit(solution)/shard_map/dot_general | solution.py:85
  381.4 0.0 reduce-scatter.2.cloned.1.call-update
  381.4 0.0 all-gather.8.cloned.1.call-start
  381.5 186.5 %reduce-scatter.2.cloned.1.call-done = f32[512,4096]{1,0:T(8,128)} async-done(((f32[1024,4096]{1,0:T(8,128)}), f32[512,4096]{1,0:T(8,128)}) %reduce-scatter.2.cloned.1.call-update) | async-done | bytes 8388624 | tf_op jit(solution)/shard_map/reduce_scatter | solution.py:86
  567.9 8.0 %add_convert_fusion = bf16[512,4096]{1,0:T(8,128)(2,1)} fusion(f32[512,4096]{1,0:T(8,128)} %reduce-scatter.2.cloned.1.call-done, bf16[1024,4096]{1,0:T(8,128)(2,1)} %param.9, s32[]{:T(128)S(6)} %select_n.25), kind=kLoop, calls=%fused_computation.34 | loop fusion | flops 6291456 | bytes 16777220 | tf_op jit(solution)/shard_map/convert_element_type | solution.py:89
  575.9 0.0 copy-start.2
  575.9 0.0 all-gather.8.cloned.1.call-update
  576.0 1.2 copy-done.2
  577.2 1.4 copy.47
  578.6 99.8 %all-gather.8.cloned.1.call-done = bf16[1024,4096]{1,0:T(8,128)(2,1)} async-done(((bf16[512,4096]{1,0:T(8,128)(2,1)}), bf16[1024,4096]{1,0:T(8,128)(2,1)}) %all-gather.8.cloned.1.call-update) | async-done | bytes 8388624 | tf_op jit(solution)/shard_map/all_gather | solution.py:90
  678.4 7.9 %copy.66 = bf16[1024,4096]{1,0:T(8,128)(2,1)} copy(bf16[1024,4096]{1,0:T(8,128)(2,1)} %all-gather.8.cloned.1.call-done) | data formatting | bytes 16777216
  (9 shorter events, 0.1 us)
Async XLA Ops:
  7.2 107.8 %all-gather.4.cloned.1.call-start = ((), (), s32[]{:S(2)}) async-start(), calls=%async_computation.1 | async-start | bytes 5242880 | tf_op jit(solution)/shard_map/all_gather | solution.py:81
  7.9 5.8 copy-start
  21.8 3.6 copy-start.3
  32.4 87.3 %all-gather.6.cloned.1.call-start = ((), (), s32[]{:S(2)}) async-start(), calls=%async_computation.2 | async-start | bytes 5242880 | tf_op jit(solution)/shard_map/all_gather | solution.py:82
  41.9 25.6 %copy-start.1 = (bf16[1024,512]{0,1:T(8,128)(2,1)}, bf16[1024,512]{0,1:T(8,128)(2,1)S(1)}, u32[]{:S(2)}) copy-start(bf16[1024,512]{0,1:T(8,128)(2,1)S(1)} %convolution_convert_fusion) | copy-start | bytes 3145732
  43.3 524.7 %reduce-scatter.2.cloned.1.call-start = ((), (), s32[]{:S(2)}) async-start(), calls=%async_computation.3 | async-start | bytes 25165824 | tf_op jit(solution)/shard_map/reduce_scatter | solution.py:86
  381.4 297.0 %all-gather.8.cloned.1.call-start = ((), (), s32[]{:S(2)}) async-start(), calls=%async_computation.4 | async-start | bytes 12582912 | tf_op jit(solution)/shard_map/all_gather | solution.py:90
  575.9 1.2 copy-start.2
Sparse Core Ops, SparseCore 0:
  32.5 34.3 all-gather.3
  69.0 31.4 all-gather.5
  381.5 186.3 reduce-scatter.1
  576.1 102.2 all-gather.7
where the time goes:
time: 706 us; the launch traced here: 693 us
  waiting for transfers between devices  286 us (41%)
  matrix products  284 us (40%)
  local copies, waits for them, and re-layouts  62.4 us (9%)
  other arithmetic  35.5 us (5%)
  between operations  14.3 us (2%)
  blocking collectives  10.2 us (1%)
    reduce_scatter x1, waiting for transfers between devices, device_fn(): summed = lax.psum_scatter(part_out, 'tp', scatter_dimension=0, tiled=True)  186 us
    sub x4, matrix products, one_block(): prob_bf = jax.nn.softmax(scores, axis=-1).astype(jnp.bfloat16)  124 us
    all_gather x1, waiting for transfers between devices, device_fn(): y_out = lax.all_gather(y_share, 'tp', axis=0, tiled=True)  99.8 us
    dot_general x4, matrix products, one_block(): jnp.einsum('qhgt,thd->qhgd', prob_bf, values, preferred_element_type=jnp....  95.9 us
    dot_general x1, matrix products, device_fn(): jnp.dot(hidden, w_q, preferred_element_type=jnp.float32)  24.2 us
    dot_general x1, matrix products, device_fn(): part_out = jnp.dot(attn, w_o, preferred_element_type=jnp.float32)  23.7 us
    unnamed x12, local copies, waits for them, and re-layouts  14.7 us
  transfers between devices with their start and end apart: 4, of which 2 were waited for; matrix products, arithmetic and copies ran while one was open for 11% of the time, Pallas kernels for 0%

commit v1 on v0

v1 whole, which is shorter than its diff:
```python
import math
import functools
import numpy as np
import jax
import jax.numpy as jnp
from jax import lax
from jax.experimental import pallas as pl
from jax.experimental.pallas import tpu as pltpu
from jax.sharding import PartitionSpec as P

HEAD_DIM = 128
NORM_EPS = 1e-5
SCALE_LOG2 = (1.0 / math.sqrt(HEAD_DIM)) * math.log2(math.e)
N_CP = 4
MESH = pl.DeviceIdType.MESH
BF16 = jnp.bfloat16
F32 = jnp.float32


def rope_freqs():
    exponent = np.arange(0, HEAD_DIM, 2) / HEAD_DIM
    base_freq = 1.0 / (500000.0 ** exponent)
    wave_len = 2.0 * math.pi / base_freq
    smooth = (8192.0 / wave_len - 1.0) / 3.0
    blended = (1.0 - smooth) * base_freq / 8.0 + smooth * base_freq
    freqs = np.where(wave_len < 2048.0, base_freq, np.where(wave_len > 8192.0, base_freq / 8.0, blended))
    return freqs.astype(np.float32)


def layer_kernel(x_hbm, pos_ref, freq_ref, gain_ref, wq_hbm, wk_hbm, wv_hbm, wo_hbm,
                 y_hbm, kf_hbm, vf_hbm, w1_hbm,
                 hbuf, wbuf, xbuf, kv_ref, qt_ref, s_even, s_odd, p_even, p_odd,
                 m_ref, l_ref, att_ref, acc_ref, kst_ref, vst_ref, cos_t, sin_t, cos_f, sin_f,
                 x_sem, w_sem, f_sem, y_sem,
                 wy_s, wy_r, wx_s, wx_r, wc_s, wc_r, wd_s, wd_r,
                 kc_s, kc_r, kx_s, kx_r, kd_s, kd_r, oy_s, oy_r, or_s, or_r, free_sem):
    rows, dim = hbuf.shape
    width = wk_hbm.shape[1]
    n_grp = wq_hbm.shape[1] // width
    own_cols = n_grp * width
    seg = rows // 2
    half = HEAD_DIM // 2
    blk = 256
    n_blk = rows // blk
    heads = width // HEAD_DIM
    me = lax.axis_index("cp")
    peer_y = {"tp": 1 - lax.axis_index("tp")}
    peer_c = {"cp": me + 1 - 2 * (me % 2)}
    peer_x = {"cp": (me + 2) % N_CP}
    s_refs, p_refs = (s_even, s_odd), (p_even, p_odd)

    def at(i, size):
        return pl.ds(pl.multiple_of(i * size, size), size)

    def remote(src, dst, send, recv, peer):
        return pltpu.make_async_remote_copy(src_ref=src, dst_ref=dst, send_sem=send, recv_sem=recv,
                                            device_id=peer, device_id_type=MESH)

    def w_rows(g, owner):
        return pl.ds(pl.multiple_of(g * width + owner * HEAD_DIM, HEAD_DIM), HEAD_DIM)

    other_x = (me + 2) % N_CP

    def wy(g):
        return remote(wo_hbm.at[w_rows(g, me)], w1_hbm.at[w_rows(g, me)], wy_s.at[g], wy_r.at[g], peer_y)

    def wx(g):
        return remote(w1_hbm.at[w_rows(g, me)], w1_hbm.at[w_rows(g, me)], wx_s.at[g], wx_r.at[g], peer_x)

    def wc(g):
        return remote(w1_hbm.at[w_rows(g, me)], w1_hbm.at[w_rows(g, me)], wc_s.at[g], wc_r.at[g], peer_c)

    def wd(g):
        return remote(w1_hbm.at[w_rows(g, other_x)], w1_hbm.at[w_rows(g, other_x)], wd_s.at[g], wd_r.at[g], peer_c)

    def kc():
        return remote(kv_ref.at[0], kv_ref.at[1], kc_s, kc_r, peer_c)

    def kx(n):
        return remote(kv_ref.at[0, n], kv_ref.at[2, n], kx_s.at[n], kx_r.at[n], peer_x)

    def kd(n):
        return remote(kv_ref.at[2, n], kv_ref.at[3, n], kd_s.at[n], kd_r.at[n], peer_c)

    def oy(g):
        return remote(hbuf.at[:, at(g, width)], hbuf.at[:, at(g + n_grp, width)], oy_s.at[g], oy_r.at[g], peer_y)

    def o_last(r):
        g = n_grp - 1
        return remote(hbuf.at[at(r, blk), at(g, width)], hbuf.at[at(r, blk), at(g + n_grp, width)],
                      or_s.at[r], or_r.at[r], peer_y)

    def x_in(r):
        return pltpu.make_async_copy(x_hbm.at[at(r, blk)], xbuf.at[r % 2], x_sem.at[r % 2])

    def q_in(g):
        return pltpu.make_async_copy(wq_hbm.at[:, at(g, width)], wbuf.at[g % 2], w_sem.at[g % 2])

    def o_tile(j):
        return wbuf.at[(j % 4) // 2, at(j % 2, own_cols)]

    def o_in(j):
        return pltpu.make_async_copy(wo_hbm.at[:, at(j, width)], o_tile(j), w_sem.at[j % 4])

    n_tile = dim // width

    def w1_in(g, j):
        return pltpu.make_async_copy(w1_hbm.at[at(g, width), at(j, width)], wbuf.at[g % 2, at(j, width)], f_sem.at[g % 2, j])

    def y_out(r):
        return pltpu.make_async_copy(xbuf.at[r % 2], y_hbm.at[at(r, blk)], y_sem.at[r % 2])

    k_in = pltpu.make_async_copy(wk_hbm, wbuf.at[0], w_sem.at[0])
    v_in = pltpu.make_async_copy(wv_hbm, wbuf.at[1], w_sem.at[1])
    k_out = pltpu.make_async_copy(kst_ref, kf_hbm, y_sem.at[0])
    v_out = pltpu.make_async_copy(vst_ref, vf_hbm, y_sem.at[1])

    x_in(0).start()
    k_in.start()
    x_in(1).start()
    v_in.start()
    barrier = pltpu.get_barrier_semaphore()
    for peer in (peer_y, peer_c, peer_x):
        pl.semaphore_signal(barrier, inc=1, device_id=peer, device_id_type=MESH)
    pl.semaphore_wait(barrier, 3)
    wy(0).start()
    wy(1).start()

    def trig(c, carry):
        cols = at(c, blk)
        angle = freq_ref[...] * pos_ref[:, cols].astype(F32)
        turns = jnp.floor(angle * (0.5 / math.pi) + 0.5)
        angle = ((angle - turns * 6.28125) - turns * 1.9350051879882812e-03) - turns * 3.0199159819e-07
        cosine, sine = jnp.cos(angle), jnp.sin(angle)
        cos_t[:, cols] = cosine
        sin_t[:, cols] = sine
        cos_f[cols, :] = jnp.concatenate([cosine, cosine], axis=0).T
        sin_f[cols, :] = jnp.concatenate([-sine, sine], axis=0).T
        return carry

    lax.fori_loop(0, n_blk, trig, 0)

    k_in.wait()

    def norm_k(r, carry):
        x_in(r).wait()
        rws = at(r, blk)
        x = xbuf[r % 2].astype(F32)
        acc_ref[rws, :] = x
        normed = x * lax.rsqrt(jnp.mean(x * x, axis=-1, keepdims=True) + NORM_EPS)
        h = (normed * gain_ref[...].astype(F32)).astype(BF16)
        hbuf[rws, :] = h

        @pl.when(r < n_blk - 2)
        def _():
            x_in(r + 2).start()

        k = jnp.dot(h, wbuf[0], preferred_element_type=F32).astype(BF16)
        for n in range(heads):
            vec = k[:, n * HEAD_DIM:(n + 1) * HEAD_DIM].astype(F32)
            rot = (vec * cos_f[rws, :] + pltpu.roll(vec, half, 1) * sin_f[rws, :]).astype(BF16)
            kst_ref[rws, n * HEAD_DIM:(n + 1) * HEAD_DIM] = rot
            kv_ref[0, n, 0, rws, :] = rot
        return carry

    lax.fori_loop(0, n_blk, norm_k, 0)
    q_in(0).start()
    v_in.wait()

    def proj_v(r, carry):
        rws = at(r, blk)
        v = jnp.dot(hbuf[rws, :], wbuf[1], preferred_element_type=F32).astype(BF16)
        vst_ref[rws, :] = v
        for n in range(heads):
            for b in range(blk // HEAD_DIM):
                square = v[b * HEAD_DIM:(b + 1) * HEAD_DIM, n * HEAD_DIM:(n + 1) * HEAD_DIM].astype(F32).T.astype(BF16)
                kv_ref[0, n, 1, pl.ds(pl.multiple_of(r * blk + b * HEAD_DIM, HEAD_DIM), HEAD_DIM), :] = square
        return carry

    lax.fori_loop(0, n_blk, proj_v, 0)
    q_in(1).start()

    def proj_q(g, carry):
        q_in(g).wait()

        def rows_q(r, inner):
            rws = at(r, blk)
            q = jnp.dot(hbuf[rws, :], wbuf[g % 2], preferred_element_type=F32).astype(BF16)
            for n in range(heads):
                vec = q[:, n * HEAD_DIM:(n + 1) * HEAD_DIM].astype(F32).T
                a, b = vec[:half], vec[half:]
                out = jnp.concatenate([a * cos_t[:, rws] - b * sin_t[:, rws], b * cos_t[:, rws] + a * sin_t[:, rws]], axis=0)
                qt_ref[pl.ds(pl.multiple_of(g * width + n * HEAD_DIM, HEAD_DIM), HEAD_DIM), rws] = out.astype(BF16)

            @pl.when(jnp.logical_and(g == 0, r == 0))
            def _():
                kc().start()
                kx(0).start()
                k_out.start()
                v_out.start()
            return inner

        lax.fori_loop(0, n_blk, rows_q, 0)

        @pl.when(g < n_grp - 2)
        def _():
            q_in(g + 2).start()

        @pl.when(g == 1)
        def _():
            kx(1).start()
        return carry

    lax.fori_loop(0, n_grp, proj_q, 0)
    kx(2).start()
    pl.semaphore_signal(free_sem, inc=1, device_id=peer_y, device_id_type=MESH)
    for j in range(4):
        o_in(j).start()
    kc().wait()
    k_out.wait()
    v_out.wait()

    def attention(g, outer):
        kx(g).wait_recv()
        kd(g).start()

        @pl.when(g == 1)
        def _():
            kx(3).start()

        m_ref[...] = jnp.full_like(m_ref, -1e30)
        l_ref[...] = jnp.zeros_like(l_ref)
        att_ref[...] = jnp.zeros_like(att_ref)

        def scores(q_half, src, k_half, n, slot, diagonal):
            k = kv_ref[src, g, 0, at(k_half, seg), :]
            q = qt_ref[pl.ds(pl.multiple_of(g * width + n * HEAD_DIM, HEAD_DIM), HEAD_DIM), at(q_half, seg)]
            s = jnp.dot(k, q, preferred_element_type=F32)
            if diagonal:
                keep = lax.broadcasted_iota(jnp.int32, (seg, seg), 0) <= lax.broadcasted_iota(jnp.int32, (seg, seg), 1)
                s = jnp.where(keep, s, -1e30)
            s_refs[slot][...] = s
            return jnp.max(s.reshape(seg // 8, 8, seg), axis=0)

        def soften(q_half, n, slot, top):
            chunk = 64
            m_old = m_ref[q_half, n:n + 1, :]
            m_new = jnp.maximum(m_old, jnp.max(top, axis=0, keepdims=True))
            alpha = jnp.exp2((m_old - m_new) * SCALE_LOG2)
            shift = jnp.broadcast_to(m_new * SCALE_LOG2, (8, seg))
            m_ref[q_half, n:n + 1, :] = m_new
            total = jnp.zeros((8, seg), F32)
            for c in range(0, seg, chunk):
                s = s_refs[slot][c:c + chunk, :].reshape(chunk // 8, 8, seg)
                p = jnp.exp2(s * SCALE_LOG2 - shift[None])
                total = total + jnp.sum(p, axis=0)
                p_refs[slot][c:c + chunk, :] = p.reshape(chunk, seg).astype(BF16)
            l_ref[q_half, n:n + 1, :] = l_ref[q_half, n:n + 1, :] * alpha + jnp.sum(total, axis=0, keepdims=True)
            return alpha

        def weigh(q_half, src, k_half, n, slot, alpha):
            v_t = jnp.concatenate([kv_ref[src, g, 1, pl.ds(pl.multiple_of(k_half * seg + b, HEAD_DIM), HEAD_DIM), :]
                                   for b in range(0, seg, HEAD_DIM)], axis=1)
            rws = slice(n * HEAD_DIM, (n + 1) * HEAD_DIM)
            att_ref[q_half, rws, :] = att_ref[q_half, rws, :] * alpha + jnp.dot(
                v_t, p_refs[slot][...], preferred_element_type=F32)

        def block(q_half, src, k_half, top, following):
            previous = None
            for n in range(heads):
                if n + 1 < heads:
                    top_next = scores(q_half, src, k_half, n + 1, (n + 1) % 2, following is None)
                else:
                    top_next = None if following is None else scores(*following, 0, 0, False)
                alpha = soften(q_half, n, n % 2, top)
                if previous is not None:
                    weigh(*previous)
                previous = (q_half, src, k_half, n, n % 2, alpha)
                top = top_next
            weigh(*previous)
            return top

        def place(step):
            src = (step + 1) // 2
            near = 1 - src // 2
            lower = near * (me % 2) + (1 - near) * (me // 2)
            free = (1 - step % 2) * ((step + 6) // 7)
            return 1 - free * lower, src, free * (1 - lower)

        def on_diagonal(side, carry):
            block(side, 0, side, scores(side, 0, side, 0, 0, True), None)
            return carry

        lax.fori_loop(0, 2, on_diagonal, 0)
        kd(g).wait_recv()
        n_steps = 7

        def step_body(step, top):
            @pl.when(jnp.logical_and(g == 0, step == 5))
            def _():
                wy(2).start()
                wy(3).start()

            @pl.when(jnp.logical_and(g == 1, step == 2))
            def _():
                for w in (0, 1):
                    wy(w).wait_recv()
                    wx(w).start()
                    wc(w).start()

            @pl.when(jnp.logical_and(g == 3, step == 4))
            def _():
                pl.semaphore_wait(free_sem, 1)
                oy(0).start()
                oy(1).start()

            return block(*place(step), top, place(jnp.minimum(step + 1, n_steps - 1)))

        lax.fori_loop(0, n_steps, step_body, scores(*place(0), 0, 0, False))

        def write(q_half, carry):
            for n in range(heads):
                o = (att_ref[q_half, n * HEAD_DIM:(n + 1) * HEAD_DIM, :] / l_ref[q_half, n:n + 1, :]).T.astype(BF16)
                hbuf[at(q_half, seg), pl.ds(pl.multiple_of(g * width + n * HEAD_DIM, HEAD_DIM), HEAD_DIM)] = o
            return carry

        lax.fori_loop(0, 2, write, 0)
        return outer

    lax.fori_loop(0, n_grp, attention, 0)

    def out_own(j, carry):
        o_in(j).wait()

        def add(r, inner):
            acc_ref[at(r, blk), at(j, width)] += jnp.dot(hbuf[at(r, blk), 0:own_cols], o_tile(j)[...], preferred_element_type=F32)
            return inner

        lax.fori_loop(0, n_blk, add, 0)

        @pl.when(j < n_tile - 4)
        def _():
            o_in(j + 4).start()

        @pl.when(j == 1)
        def _():
            for w in (2, 3):
                wy(w).wait_recv()
                wx(w).start()
                wc(w).start()

        @pl.when(j == 5)
        def _():
            for w in (0, 1):
                wx(w).wait_recv()
                wd(w).start()

        @pl.when(j == 6)
        def _():
            oy(2).start()
        return carry

    lax.fori_loop(0, n_tile, out_own, 0)

    def load_group(g):
        wc(g).wait_recv()
        wd(g).wait_recv()
        for j in range(n_tile):
            w1_in(g, j).start()

    def add_group(g, r):
        def add(j, carry):
            acc_ref[at(r, blk), at(j, width)] += jnp.dot(
                hbuf[at(r, blk), at(g + n_grp, width)], wbuf[g % 2, at(j, width)], preferred_element_type=F32)
            return carry

        lax.fori_loop(0, n_tile, add, 0)

    def add_rows(g):
        def body(r, carry):
            add_group(g, r)
            return carry

        lax.fori_loop(0, n_blk, body, 0)

    load_group(0)
    load_group(1)
    oy(0).wait_recv()
    o_last(0).start()
    for j in range(n_tile):
        w1_in(0, j).wait()
    add_rows(0)
    oy(1).wait_recv()
    o_last(1).start()
    for w in (2, 3):
        wx(w).wait_recv()
        wd(w).start()
    for j in range(n_tile):
        w1_in(1, j).wait()
    add_rows(1)
    load_group(2)
    load_group(3)
    o_last(2).start()
    oy(2).wait_recv()
    for j in range(n_tile):
        w1_in(2, j).wait()
    add_rows(2)
    o_last(3).start()
    for j in range(n_tile):
        w1_in(3, j).wait()

    def finish(r, carry):
        o_last(r).wait_recv()
        add_group(n_grp - 1, r)

        @pl.when(r >= 2)
        def _():
            y_out(r - 2).wait()

        xbuf[r % 2] = acc_ref[at(r, blk), :].astype(BF16)
        y_out(r).start()
        return carry

    lax.fori_loop(0, n_blk, finish, 0)
    y_out(n_blk - 2).wait()
    y_out(n_blk - 1).wait()

    for n in range(4):
        kx(n).wait_send()
        kd(n).wait_send()
        wy(n).wait_send()
        wx(n).wait_send()
        wc(n).wait_send()
        wd(n).wait_send()
        o_last(n).wait_send()
    for g in range(3):
        oy(g).wait_send()


def write_kernel(y_ref, k_ref, v_ref, y_out, k_out, v_out):
    y_out[...] = y_ref[...]
    for n in range(k_out.shape[1]):
        k_out[:, n, :] = k_ref[:, n * HEAD_DIM:(n + 1) * HEAD_DIM]
        v_out[:, n, :] = v_ref[:, n * HEAD_DIM:(n + 1) * HEAD_DIM]


def solution(mesh):
    def device_fn(x_in, positions, norm_gain, w_q, w_k, w_v, w_o):
        rows, dim = x_in.shape
        cols = w_k.shape[1]
        kv_dev = cols // HEAD_DIM
        seg = rows // 2
        half = HEAD_DIM // 2
        hbm = pl.BlockSpec(memory_space=pl.ANY)
        vmem = pl.BlockSpec(memory_space=pltpu.VMEM)
        dma = pltpu.SemaphoreType.DMA
        y_raw, k_flat, v_flat, _ = pl.pallas_call(
            layer_kernel,
            in_specs=[hbm, vmem, vmem, vmem, hbm, hbm, hbm, hbm],
            out_specs=[hbm] * 4,
            out_shape=[
                jax.ShapeDtypeStruct((rows, dim), BF16),
                jax.ShapeDtypeStruct((rows, cols), BF16),
                jax.ShapeDtypeStruct((rows, cols), BF16),
                jax.ShapeDtypeStruct(w_o.shape, BF16),
            ],
            scratch_shapes=[
                pltpu.VMEM((rows, dim), BF16),
                pltpu.VMEM((2, dim, cols), BF16),
                pltpu.VMEM((2, 256, dim), BF16),
                pltpu.VMEM((4, kv_dev, 2, rows, HEAD_DIM), BF16),
                pltpu.VMEM((w_q.shape[1], rows), BF16),
                pltpu.VMEM((seg, seg), F32),
                pltpu.VMEM((seg, seg), F32),
                pltpu.VMEM((seg, seg), BF16),
                pltpu.VMEM((seg, seg), BF16),
                pltpu.VMEM((2, 8, seg), F32),
                pltpu.VMEM((2, 8, seg), F32),
                pltpu.VMEM((2, cols, seg), F32),
                pltpu.VMEM((rows, dim), F32),
                pltpu.VMEM((rows, cols), BF16),
                pltpu.VMEM((rows, cols), BF16),
                pltpu.VMEM((half, rows), F32),
                pltpu.VMEM((half, rows), F32),
                pltpu.VMEM((rows, HEAD_DIM), F32),
                pltpu.VMEM((rows, HEAD_DIM), F32),
                dma((2,)), dma((4,)), dma((2, 8)), dma((2,)),
                dma((4,)), dma((4,)), dma((4,)), dma((4,)), dma((4,)), dma((4,)), dma((4,)), dma((4,)),
                dma, dma, dma((4,)), dma((4,)), dma((4,)), dma((4,)),
                dma((3,)), dma((3,)), dma((4,)), dma((4,)),
                pltpu.SemaphoreType.REGULAR,
            ],
            compiler_params=pltpu.CompilerParams(collective_id=0, has_side_effects=True, vmem_limit_bytes=67043328),
            name="layer",
        )(x_in, positions.reshape(1, rows), jnp.asarray(rope_freqs())[:, None], norm_gain.reshape(1, dim), w_q, w_k, w_v, w_o)
        blk = 128
        return pl.pallas_call(
            write_kernel,
            grid=(rows // blk,),
            in_specs=[pl.BlockSpec((blk, dim), lambda i: (i, 0))] + [pl.BlockSpec((blk, cols), lambda i: (i, 0))] * 2,
            out_specs=[pl.BlockSpec((blk, dim), lambda i: (i, 0))] + [pl.BlockSpec((blk, kv_dev, HEAD_DIM), lambda i: (i, 0, 0))] * 2,
            out_shape=[jax.ShapeDtypeStruct((rows, dim), BF16)] + [jax.ShapeDtypeStruct((rows, kv_dev, HEAD_DIM), BF16)] * 2,
            name="write",
        )(y_raw, k_flat, v_flat)

    row_spec = P(('dp', 'cp'), None)
    cache_spec = P(('dp', 'cp'), 'tp', None)
    return jax.shard_map(device_fn, mesh=mesh, in_specs=(row_spec, P(('dp', 'cp')), P(None), P(None, 'tp'), P(None, 'tp'), P(None, 'tp'), P('tp', None)), out_specs=(row_spec, cache_spec, cache_spec), check_vma=False)
```

time: 706 us -> 208 us (0.29); the launches traced: 693 us -> 208 us
  waiting for transfers between devices: 286 us -> 0 us
  matrix products: 284 us -> 0 us
  Pallas kernels: 0 us -> 206 us
  local copies, waits for them, and re-layouts: 62.4 us -> 1.31 us
  other arithmetic: 35.5 us -> 0 us
  between operations: 14.3 us -> 0.64 us
  blocking collectives: 10.2 us -> 0 us
    pallas_call x0 -> x2, Pallas kernels: none -> 206 us  [the longest x1 194 us: device_fn(): pl.pallas_call(layer_kernel, in_specs=[hbm, vmem, vmem, vmem, hbm, hbm, h...]
    reduce_scatter x1 -> x0, waiting for transfers between devices: 186 us -> none  [device_fn(): summed = lax.psum_scatter(part_out, 'tp', scatter_dimension=0, tiled=True)]
    dot_general x8 -> x0, matrix products: 160 us -> none  [the longest x4 95.9 us: one_block(): jnp.einsum('qhgt,thd->qhgd', prob_bf, values, preferred_element_type=jnp....]
    sub x4 -> x0, matrix products: 124 us -> none  [one_block(): prob_bf = jax.nn.softmax(scores, axis=-1).astype(jnp.bfloat16)]
    all_gather x3 -> x0, waiting for transfers between devices: 99.8 us -> none  [the longest x1 99.8 us: device_fn(): y_out = lax.all_gather(y_share, 'tp', axis=0, tiled=True)]
    unnamed x12 -> x0, local copies, waits for them, and re-layouts: 14.7 us -> none
    while x2 -> x0, local copies, waits for them, and re-layouts: 12.3 us -> none  [attend_all(): o_blocks = lax.map(one_block, (q_blocks, pos_blocks))]
    all_gather x1 -> x0, blocking collectives: 10.2 us -> none  [device_fn(): pos_all = lax.all_gather(positions, 'cp', axis=0, tiled=True)]
  transfers between devices with their start and end apart: 4 -> 0, of which waited for: 2 -> 0; matrix products, arithmetic and copies ran while one was open for 11% -> 0% of each run, Pallas kernels for 0% -> 0%
where the time goes in v1:
time: 208 us
  Pallas kernels  206 us (99%)
    pallas_call x1, Pallas kernels, device_fn(): pl.pallas_call(layer_kernel, in_specs=[hbm, vmem, vmem, vmem, hbm, hbm, h...  194 us
    pallas_call x1, Pallas kernels, device_fn(): pl.pallas_call(write_kernel, grid=(rows // blk,), in_specs=[pl.BlockSpec(...  11.6 us

profile of v1, /device:TPU:0, one launch (start us, length us, event | category | flops | bytes accessed | tf_op | source)
XLA Modules:
  0.0 207.8 jit_solution(1648440408980820865)
XLA Ops:
  0.6 1.3 reshape.13.gain_ref
  1.9 194.3 %layer.1 = (bf16[1024,4096]{1,0:T(8,128)(2,1)}, bf16[1024,512]{1,0:T(8,128)(2,1)}, bf16[1024,512]{1,0:T(8,128)(2,1)}, bf16[2048,4096]{1,0:T(8,128)(2,1)}) custom-call(bf16[1024,4096]{1,0:T(8,128)(2,1)} %x_hbm.1, s32[1,1024]{1,0:T(1,128)} %bitcast.1, f32[64,1]{1,0:T(8,128)} %constant.3.freq_ref, bf16[1,4096]{1,0:T(2,128)(2,1)} %reshape.13.gain_ref, ...), custom_call_target="tpu_custom_call" | custom-call | tf_op jit(solution)/shard_map/layer/pallas_call | solution.py:457
  196.3 11.6 %write.1 = (bf16[1024,4096]{1,0:T(8,128)(2,1)}, bf16[1024,4,128]{2,1,0:T(4,128)(2,1)}, bf16[1024,4,128]{2,1,0:T(4,128)(2,1)}) custom-call(bf16[1024,4096]{1,0:T(8,128)(2,1)} %get-tuple-element.6.y_ref, bf16[1024,512]{1,0:T(8,128)(2,1)} %get-tuple-element.7.k_ref, bf16[1024,512]{1,0:T(8,128)(2,1)} %get-tuple-element.8.v_ref), custom_call_target="tpu_custom_call" | custom-call | tf_op jit(solution)/shard_map/write/pallas_call | solution.py:497

commit v2 on v1

--- a/solution.py
+++ b/solution.py
@@ -28,10 +28,10 @@
 
 
 def layer_kernel(x_hbm, pos_ref, freq_ref, gain_ref, wq_hbm, wk_hbm, wv_hbm, wo_hbm,
-                 y_hbm, kf_hbm, vf_hbm, w1_hbm,
-                 hbuf, wbuf, xbuf, kv_ref, qt_ref, s_even, s_odd, p_even, p_odd,
-                 m_ref, l_ref, att_ref, acc_ref, kst_ref, vst_ref, cos_t, sin_t, cos_f, sin_f,
-                 x_sem, w_sem, f_sem, y_sem,
+                 y_ref, kst_ref, vst_ref, w1_hbm,
+                 hbuf, wbuf, kv_ref, qt_ref, s_even, s_odd, p_even, p_odd,
+                 m_ref, l_ref, att_ref, acc_ref, cos_t, sin_t, gain_f,
+                 x_sem, w_sem, f_sem,
                  wy_s, wy_r, wx_s, wx_r, wc_s, wc_r, wd_s, wd_r,
                  kc_s, kc_r, kx_s, kx_r, kd_s, kd_r, oy_s, oy_r, or_s, or_r, free_sem):
     rows, dim = hbuf.shape
@@ -91,7 +91,7 @@
                       or_s.at[r], or_r.at[r], peer_y)
 
     def x_in(r):
-        return pltpu.make_async_copy(x_hbm.at[at(r, blk)], xbuf.at[r % 2], x_sem.at[r % 2])
+        return pltpu.make_async_copy(x_hbm.at[at(r, blk)], y_ref.at[at(r, blk)], x_sem.at[r])
 
     def q_in(g):
         return pltpu.make_async_copy(wq_hbm.at[:, at(g, width)], wbuf.at[g % 2], w_sem.at[g % 2])
@@ -107,24 +107,24 @@
     def w1_in(g, j):
         return pltpu.make_async_copy(w1_hbm.at[at(g, width), at(j, width)], wbuf.at[g % 2, at(j, width)], f_sem.at[g % 2, j])
 
-    def y_out(r):
-        return pltpu.make_async_copy(xbuf.at[r % 2], y_hbm.at[at(r, blk)], y_sem.at[r % 2])
-
     k_in = pltpu.make_async_copy(wk_hbm, wbuf.at[0], w_sem.at[0])
     v_in = pltpu.make_async_copy(wv_hbm, wbuf.at[1], w_sem.at[1])
-    k_out = pltpu.make_async_copy(kst_ref, kf_hbm, y_sem.at[0])
-    v_out = pltpu.make_async_copy(vst_ref, vf_hbm, y_sem.at[1])
 
     x_in(0).start()
     k_in.start()
     x_in(1).start()
     v_in.start()
+    x_in(2).start()
+    x_in(3).start()
     barrier = pltpu.get_barrier_semaphore()
     for peer in (peer_y, peer_c, peer_x):
         pl.semaphore_signal(barrier, inc=1, device_id=peer, device_id_type=MESH)
     pl.semaphore_wait(barrier, 3)
     wy(0).start()
     wy(1).start()
+
+    gain = gain_ref[...].astype(F32)
+    gain_f[...] = jnp.concatenate([gain[i:i + 1, :] for i in range(gain.shape[0])], axis=1)
 
     def trig(c, carry):
         cols = at(c, blk)
@@ -134,8 +134,9 @@
         cosine, sine = jnp.cos(angle), jnp.sin(angle)
         cos_t[:, cols] = cosine
         sin_t[:, cols] = sine
-        cos_f[cols, :] = jnp.concatenate([cosine, cosine], axis=0).T
-        sin_f[cols, :] = jnp.concatenate([-sine, sine], axis=0).T
+        full = (at(c % 2, blk), at(c // 2, HEAD_DIM))
+        s_even[full] = jnp.concatenate([cosine, cosine], axis=0).T
+        s_odd[full] = jnp.concatenate([-sine, sine], axis=0).T
         return carry
 
     lax.fori_loop(0, n_blk, trig, 0)
@@ -145,20 +146,20 @@
     def norm_k(r, carry):
         x_in(r).wait()
         rws = at(r, blk)
-        x = xbuf[r % 2].astype(F32)
-        acc_ref[rws, :] = x
-        normed = x * lax.rsqrt(jnp.mean(x * x, axis=-1, keepdims=True) + NORM_EPS)
-        h = (normed * gain_ref[...].astype(F32)).astype(BF16)
-        hbuf[rws, :] = h
-
-        @pl.when(r < n_blk - 2)
-        def _():
-            x_in(r + 2).start()
-
-        k = jnp.dot(h, wbuf[0], preferred_element_type=F32).astype(BF16)
+
+        def norm(i, inner):
+            part = pl.ds(pl.multiple_of(r * blk + i * 32, 32), 32)
+            x = y_ref[part, :].astype(F32)
+            normed = x * lax.rsqrt(jnp.mean(x * x, axis=-1, keepdims=True) + NORM_EPS)
+            hbuf[part, :] = (normed * gain_f[...]).astype(BF16)
+            return inner
+
+        lax.fori_loop(0, blk // 32, norm, 0)
+        k = jnp.dot(hbuf[rws, :], wbuf[0], preferred_element_type=F32).astype(BF16)
+        full = (at(r % 2, blk), at(r // 2, HEAD_DIM))
         for n in range(heads):
             vec = k[:, n * HEAD_DIM:(n + 1) * HEAD_DIM].astype(F32)
-            rot = (vec * cos_f[rws, :] + pltpu.roll(vec, half, 1) * sin_f[rws, :]).astype(BF16)
+            rot = (vec * s_even[full] + pltpu.roll(vec, half, 1) * s_odd[full]).astype(BF16)
             kst_ref[rws, n * HEAD_DIM:(n + 1) * HEAD_DIM] = rot
             kv_ref[0, n, 0, rws, :] = rot
         return carry
@@ -196,8 +197,6 @@
             def _():
                 kc().start()
                 kx(0).start()
-                k_out.start()
-                v_out.start()
             return inner
 
         lax.fori_loop(0, n_blk, rows_q, 0)
@@ -217,8 +216,6 @@
     for j in range(4):
         o_in(j).start()
     kc().wait()
-    k_out.wait()
-    v_out.wait()
 
     def attention(g, outer):
         kx(g).wait_recv()
@@ -333,7 +330,8 @@
         o_in(j).wait()
 
         def add(r, inner):
-            acc_ref[at(r, blk), at(j, width)] += jnp.dot(hbuf[at(r, blk), 0:own_cols], o_tile(j)[...], preferred_element_type=F32)
+            acc_ref[at(r, blk), at(j, width)] = y_ref[at(r, blk), at(j, width)].astype(F32) + jnp.dot(
+                hbuf[at(r, blk), 0:own_cols], o_tile(j)[...], preferred_element_type=F32)
             return inner
 
         lax.fori_loop(0, n_blk, add, 0)
@@ -413,17 +411,16 @@
         o_last(r).wait_recv()
         add_group(n_grp - 1, r)
 
-        @pl.when(r >= 2)
-        def _():
-            y_out(r - 2).wait()
-
-        xbuf[r % 2] = acc_ref[at(r, blk), :].astype(BF16)
-        y_out(r).start()
+
+        def round_off(i, inner):
+            part = pl.ds(pl.multiple_of(r * blk + i * 32, 32), 32)
+            y_ref[part, :] = acc_ref[part, :].astype(BF16)
+            return inner
+
+        lax.fori_loop(0, blk // 32, round_off, 0)
         return carry
 
     lax.fori_loop(0, n_blk, finish, 0)
-    y_out(n_blk - 2).wait()
-    y_out(n_blk - 1).wait()
 
     for n in range(4):
         kx(n).wait_send()
@@ -437,11 +434,19 @@
         oy(g).wait_send()
 
 
-def write_kernel(y_ref, k_ref, v_ref, y_out, k_out, v_out):
-    y_out[...] = y_ref[...]
-    for n in range(k_out.shape[1]):
-        k_out[:, n, :] = k_ref[:, n * HEAD_DIM:(n + 1) * HEAD_DIM]
-        v_out[:, n, :] = v_ref[:, n * HEAD_DIM:(n + 1) * HEAD_DIM]
+def write_kernel(y_ref, k_ref, v_ref, y_hbm, k_hbm, v_hbm, k_buf, v_buf, sem):
+    copies = [pltpu.make_async_copy(y_ref, y_hbm, sem.at[0]),
+              pltpu.make_async_copy(k_buf, k_hbm, sem.at[1]),
+              pltpu.make_async_copy(v_buf, v_hbm, sem.at[2])]
+    copies[0].start()
+    for n in range(k_buf.shape[1]):
+        k_buf[:, n, :] = k_ref[:, n * HEAD_DIM:(n + 1) * HEAD_DIM]
+    copies[1].start()
+    for n in range(k_buf.shape[1]):
+        v_buf[:, n, :] = v_ref[:, n * HEAD_DIM:(n + 1) * HEAD_DIM]
+    copies[2].start()
+    for copy in copies:
+        copy.wait()
 
 
 def solution(mesh):
@@ -457,17 +462,16 @@
         y_raw, k_flat, v_flat, _ = pl.pallas_call(
             layer_kernel,
             in_specs=[hbm, vmem, vmem, vmem, hbm, hbm, hbm, hbm],
-            out_specs=[hbm] * 4,
+            out_specs=[vmem] * 3 + [hbm],
             out_shape=[
-                jax.ShapeDtypeStruct((rows, dim), BF16),
-                jax.ShapeDtypeStruct((rows, cols), BF16),
-                jax.ShapeDtypeStruct((rows, cols), BF16),
+                pltpu.VMEM((rows, dim), BF16),
+                pltpu.VMEM((rows, cols), BF16),
+                pltpu.VMEM((rows, cols), BF16),
                 jax.ShapeDtypeStruct(w_o.shape, BF16),
             ],
             scratch_shapes=[
                 pltpu.VMEM((rows, dim), BF16),
                 pltpu.VMEM((2, dim, cols), BF16),
-                pltpu.VMEM((2, 256, dim), BF16),
                 pltpu.VMEM((4, kv_dev, 2, rows, HEAD_DIM), BF16),
                 pltpu.VMEM((w_q.shape[1], rows), BF16),
                 pltpu.VMEM((seg, seg), F32),
@@ -478,28 +482,26 @@
                 pltpu.VMEM((2, 8, seg), F32),
                 pltpu.VMEM((2, cols, seg), F32),
                 pltpu.VMEM((rows, dim), F32),
-                pltpu.VMEM((rows, cols), BF16),
-                pltpu.VMEM((rows, cols), BF16),
                 pltpu.VMEM((half, rows), F32),
                 pltpu.VMEM((half, rows), F32),
-                pltpu.VMEM((rows, HEAD_DIM), F32),
-                pltpu.VMEM((rows, HEAD_DIM), F32),
-                dma((2,)), dma((4,)), dma((2, 8)), dma((2,)),
+                pltpu.VMEM((1, dim), F32),
+                dma((4,)), dma((4,)), dma((2, 8)),
                 dma((4,)), dma((4,)), dma((4,)), dma((4,)), dma((4,)), dma((4,)), dma((4,)), dma((4,)),
                 dma, dma, dma((4,)), dma((4,)), dma((4,)), dma((4,)),
                 dma((3,)), dma((3,)), dma((4,)), dma((4,)),
                 pltpu.SemaphoreType.REGULAR,
             ],
-            compiler_params=pltpu.CompilerParams(collective_id=0, has_side_effects=True, vmem_limit_bytes=67043328),
+            compiler_params=pltpu.CompilerParams(collective_id=0, has_side_effects=True, vmem_limit_bytes=53 * 1024 * 1024),
             name="layer",
-        )(x_in, positions.reshape(1, rows), jnp.asarray(rope_freqs())[:, None], norm_gain.reshape(1, dim), w_q, w_k, w_v, w_o)
-        blk = 128
+        )(x_in, positions.reshape(1, rows), jnp.asarray(rope_freqs())[:, None], norm_gain.reshape(dim // HEAD_DIM, HEAD_DIM), w_q, w_k, w_v, w_o)
+        cache = jax.ShapeDtypeStruct((rows, kv_dev, HEAD_DIM), BF16)
         return pl.pallas_call(
             write_kernel,
-            grid=(rows // blk,),
-            in_specs=[pl.BlockSpec((blk, dim), lambda i: (i, 0))] + [pl.BlockSpec((blk, cols), lambda i: (i, 0))] * 2,
-            out_specs=[pl.BlockSpec((blk, dim), lambda i: (i, 0))] + [pl.BlockSpec((blk, kv_dev, HEAD_DIM), lambda i: (i, 0, 0))] * 2,
-            out_shape=[jax.ShapeDtypeStruct((rows, dim), BF16)] + [jax.ShapeDtypeStruct((rows, kv_dev, HEAD_DIM), BF16)] * 2,
+            in_specs=[vmem] * 3,
+            out_specs=[hbm] * 3,
+            out_shape=[jax.ShapeDtypeStruct((rows, dim), BF16), cache, cache],
+            scratch_shapes=[pltpu.VMEM(cache.shape, BF16), pltpu.VMEM(cache.shape, BF16), dma((3,))],
+            compiler_params=pltpu.CompilerParams(vmem_limit_bytes=16 * 1024 * 1024),
             name="write",
         )(y_raw, k_flat, v_flat)
 

time: 208 us -> 208 us (level)
    pallas_call x1, Pallas kernels: 194 us -> 197 us  [device_fn(): pl.pallas_call(layer_kernel, in_specs=[hbm, vmem, vmem, vmem, hbm, hbm, h...]
where the time goes in v2:
time: 208 us
  Pallas kernels  207 us (100%)
    pallas_call x1, Pallas kernels, device_fn(): pl.pallas_call(layer_kernel, in_specs=[hbm, vmem, vmem, vmem, hbm, hbm, h...  197 us
    pallas_call x1, Pallas kernels, device_fn(): pl.pallas_call(write_kernel, in_specs=[vmem] * 3, out_specs=[hbm] * 3, ou...  10 us

profile of v2, /device:TPU:0, one launch (start us, length us, event | category | flops | bytes accessed | tf_op | source)
XLA Modules:
  0.0 207.7 jit_solution(5465206033385026550)
XLA Ops:
  0.6 196.8 %layer.1 = (bf16[1024,4096]{1,0:T(8,128)(2,1)S(1)}, bf16[1024,512]{1,0:T(8,128)(2,1)S(1)}, bf16[1024,512]{1,0:T(8,128)(2,1)S(1)}, bf16[2048,4096]{1,0:T(8,128)(2,1)}) custom-call(bf16[1024,4096]{1,0:T(8,128)(2,1)} %x_hbm.1, s32[1,1024]{1,0:T(1,128)} %bitcast.3, f32[64,1]{1,0:T(8,128)} %constant.3.freq_ref, bf16[32,128]{1,0:T(8,128)(2,1)} %bitcast.2, ...), custom_call_target="tpu_custom_call" | custom-call | tf_op jit(solution)/shard_map/layer/pallas_call | solution.py:462
  197.5 10.0 %write.1 = (bf16[1024,4096]{1,0:T(8,128)(2,1)}, bf16[1024,4,128]{2,1,0:T(4,128)(2,1)}, bf16[1024,4,128]{2,1,0:T(4,128)(2,1)}) custom-call(bf16[1024,4096]{1,0:T(8,128)(2,1)S(1)} %get-tuple-element.6.y_ref, bf16[1024,512]{1,0:T(8,128)(2,1)S(1)} %get-tuple-element.7.k_ref, bf16[1024,512]{1,0:T(8,128)(2,1)S(1)} %get-tuple-element.8.v_ref), custom_call_target="tpu_custom_call" | custom-call | tf_op jit(solution)/shard_map/write/pallas_call | solution.py:498

commit v3 on v2

--- a/solution.py
+++ b/solution.py
@@ -110,6 +110,21 @@
     k_in = pltpu.make_async_copy(wk_hbm, wbuf.at[0], w_sem.at[0])
     v_in = pltpu.make_async_copy(wv_hbm, wbuf.at[1], w_sem.at[1])
 
+    def share(w):
+        wy(w).wait_recv()
+        wx(w).start()
+        wc(w).start()
+
+    def pass_on(w):
+        wx(w).wait_recv()
+        wd(w).start()
+
+    def load_group(g):
+        wc(g).wait_recv()
+        wd(g).wait_recv()
+        for j in range(n_tile):
+            w1_in(g, j).start()
+
     x_in(0).start()
     k_in.start()
     x_in(1).start()
@@ -121,7 +136,6 @@
         pl.semaphore_signal(barrier, inc=1, device_id=peer, device_id_type=MESH)
     pl.semaphore_wait(barrier, 3)
     wy(0).start()
-    wy(1).start()
 
     gain = gain_ref[...].astype(F32)
     gain_f[...] = jnp.concatenate([gain[i:i + 1, :] for i in range(gain.shape[0])], axis=1)
@@ -160,7 +174,6 @@
         for n in range(heads):
             vec = k[:, n * HEAD_DIM:(n + 1) * HEAD_DIM].astype(F32)
             rot = (vec * s_even[full] + pltpu.roll(vec, half, 1) * s_odd[full]).astype(BF16)
-            kst_ref[rws, n * HEAD_DIM:(n + 1) * HEAD_DIM] = rot
             kv_ref[0, n, 0, rws, :] = rot
         return carry
 
@@ -171,11 +184,14 @@
     def proj_v(r, carry):
         rws = at(r, blk)
         v = jnp.dot(hbuf[rws, :], wbuf[1], preferred_element_type=F32).astype(BF16)
-        vst_ref[rws, :] = v
         for n in range(heads):
             for b in range(blk // HEAD_DIM):
                 square = v[b * HEAD_DIM:(b + 1) * HEAD_DIM, n * HEAD_DIM:(n + 1) * HEAD_DIM].astype(F32).T.astype(BF16)
                 kv_ref[0, n, 1, pl.ds(pl.multiple_of(r * blk + b * HEAD_DIM, HEAD_DIM), HEAD_DIM), :] = square
+
+        @pl.when(r == n_blk - 2)
+        def _():
+            wy(1).start()
         return carry
 
     lax.fori_loop(0, n_blk, proj_v, 0)
@@ -197,6 +213,10 @@
             def _():
                 kc().start()
                 kx(0).start()
+
+            @pl.when(jnp.logical_and(g == n_grp - 1, r == 2))
+            def _():
+                wy(2).start()
             return inner
 
         lax.fori_loop(0, n_blk, rows_q, 0)
@@ -220,10 +240,6 @@
     def attention(g, outer):
         kx(g).wait_recv()
         kd(g).start()
-
-        @pl.when(g == 1)
-        def _():
-            kx(3).start()
 
         m_ref[...] = jnp.full_like(m_ref, -1e30)
         l_ref[...] = jnp.zeros_like(l_ref)
@@ -293,23 +309,23 @@
         n_steps = 7
 
         def step_body(step, top):
-            @pl.when(jnp.logical_and(g == 0, step == 5))
+            @pl.when(jnp.logical_and(g == 0, step == 6))
             def _():
-                wy(2).start()
-                wy(3).start()
+                share(0)
 
             @pl.when(jnp.logical_and(g == 1, step == 2))
             def _():
-                for w in (0, 1):
-                    wy(w).wait_recv()
-                    wx(w).start()
-                    wc(w).start()
-
-            @pl.when(jnp.logical_and(g == 3, step == 4))
+                wy(3).start()
+
+            @pl.when(jnp.logical_and(g == 1, step == 3))
+            def _():
+                kx(3).start()
+
+            @pl.when(jnp.logical_and(g == 2, step == 6))
             def _():
                 pl.semaphore_wait(free_sem, 1)
                 oy(0).start()
-                oy(1).start()
+                share(1)
 
             return block(*place(step), top, place(jnp.minimum(step + 1, n_steps - 1)))
 
@@ -328,96 +344,87 @@
 
     def out_own(j, carry):
         o_in(j).wait()
-
-        def add(r, inner):
-            acc_ref[at(r, blk), at(j, width)] = y_ref[at(r, blk), at(j, width)].astype(F32) + jnp.dot(
-                hbuf[at(r, blk), 0:own_cols], o_tile(j)[...], preferred_element_type=F32)
-            return inner
-
-        lax.fori_loop(0, n_blk, add, 0)
+        cols = at(j, width)
+        for r in range(n_blk):
+            rws = slice(r * blk, (r + 1) * blk)
+            acc_ref[rws, cols] = y_ref[rws, cols].astype(F32) + jnp.dot(
+                hbuf[rws, 0:own_cols], o_tile(j)[...], preferred_element_type=F32)
 
         @pl.when(j < n_tile - 4)
         def _():
             o_in(j + 4).start()
 
+        @pl.when(j == 0)
+        def _():
+            pass_on(0)
+
         @pl.when(j == 1)
         def _():
-            for w in (2, 3):
-                wy(w).wait_recv()
-                wx(w).start()
-                wc(w).start()
+            oy(1).start()
+            share(2)
 
         @pl.when(j == 5)
         def _():
-            for w in (0, 1):
-                wx(w).wait_recv()
-                wd(w).start()
-
-        @pl.when(j == 6)
-        def _():
-            oy(2).start()
+            pass_on(1)
+            load_group(0)
         return carry
 
     lax.fori_loop(0, n_tile, out_own, 0)
 
-    def load_group(g):
-        wc(g).wait_recv()
-        wd(g).wait_recv()
+    def add_group(g, tick=None):
         for j in range(n_tile):
-            w1_in(g, j).start()
-
-    def add_group(g, r):
+            w1_in(g, j).wait()
+
         def add(j, carry):
-            acc_ref[at(r, blk), at(j, width)] += jnp.dot(
-                hbuf[at(r, blk), at(g + n_grp, width)], wbuf[g % 2, at(j, width)], preferred_element_type=F32)
+            for r in range(n_blk):
+                rws = slice(r * blk, (r + 1) * blk)
+                acc_ref[rws, at(j, width)] += jnp.dot(
+                    hbuf[rws, at(g + n_grp, width)], wbuf[g % 2, at(j, width)], preferred_element_type=F32)
+            if tick is not None:
+                pl.when(j == n_tile // 2)(tick)
             return carry
 
         lax.fori_loop(0, n_tile, add, 0)
 
-    def add_rows(g):
-        def body(r, carry):
-            add_group(g, r)
-            return carry
-
-        lax.fori_loop(0, n_blk, body, 0)
-
-    load_group(0)
     load_group(1)
     oy(0).wait_recv()
+    add_group(0, lambda: oy(2).start())
+    share(3)
+    oy(1).wait_recv()
+    add_group(1)
+    pass_on(2)
     o_last(0).start()
-    for j in range(n_tile):
-        w1_in(0, j).wait()
-    add_rows(0)
-    oy(1).wait_recv()
+
+    def caches(c, carry):
+        rws = at(c, HEAD_DIM)
+        for n in range(heads):
+            kst_ref[rws, n, :] = kv_ref[0, n, 0, rws, :]
+            vst_ref[rws, n, :] = kv_ref[0, n, 1, rws, :].astype(F32).T.astype(BF16)
+        return carry
+
+    lax.fori_loop(0, rows // HEAD_DIM, caches, 0)
+    load_group(2)
+    o_last(0).wait_recv()
     o_last(1).start()
-    for w in (2, 3):
-        wx(w).wait_recv()
-        wd(w).start()
-    for j in range(n_tile):
-        w1_in(1, j).wait()
-    add_rows(1)
-    load_group(2)
+    pass_on(3)
+    oy(2).wait_recv()
+    o_last(2).start()
     load_group(3)
-    o_last(2).start()
-    oy(2).wait_recv()
-    for j in range(n_tile):
-        w1_in(2, j).wait()
-    add_rows(2)
-    o_last(3).start()
+    add_group(2, lambda: o_last(3).start())
     for j in range(n_tile):
         w1_in(3, j).wait()
 
     def finish(r, carry):
-        o_last(r).wait_recv()
-        add_group(n_grp - 1, r)
-
-
-        def round_off(i, inner):
-            part = pl.ds(pl.multiple_of(r * blk + i * 32, 32), 32)
-            y_ref[part, :] = acc_ref[part, :].astype(BF16)
-            return inner
-
-        lax.fori_loop(0, blk // 32, round_off, 0)
+        @pl.when(r > 0)
+        def _():
+            o_last(r).wait_recv()
+
+        rws = at(r, blk)
+        for j in range(n_tile):
+            cols = slice(j * width, (j + 1) * width)
+            total = acc_ref[rws, cols] + jnp.dot(hbuf[rws, at(2 * n_grp - 1, width)], wbuf[1, at(j, width)],
+                                                 preferred_element_type=F32)
+            y_ref[rws, cols] = total.astype(BF16)
         return carry
 
     lax.fori_loop(0, n_blk, finish, 0)
@@ -434,17 +441,17 @@
         oy(g).wait_send()
 
 
-def write_kernel(y_ref, k_ref, v_ref, y_hbm, k_hbm, v_hbm, k_buf, v_buf, sem):
-    copies = [pltpu.make_async_copy(y_ref, y_hbm, sem.at[0]),
-              pltpu.make_async_copy(k_buf, k_hbm, sem.at[1]),
-              pltpu.make_async_copy(v_buf, v_hbm, sem.at[2])]
-    copies[0].start()
-    for n in range(k_buf.shape[1]):
-        k_buf[:, n, :] = k_ref[:, n * HEAD_DIM:(n + 1) * HEAD_DIM]
-    copies[1].start()
-    for n in range(k_buf.shape[1]):
-        v_buf[:, n, :] = v_ref[:, n * HEAD_DIM:(n + 1) * HEAD_DIM]
-    copies[2].start()
+def write_kernel(y_ref, k_ref, v_ref, y_hbm, k_hbm, v_hbm, sem):
+    pieces = 8
+    size = y_ref.shape[0] // pieces
+    copies = []
+    for i in range(pieces):
+        part = pl.ds(i * size, size)
+        copies.append(pltpu.make_async_copy(y_ref.at[part], y_hbm.at[part], sem.at[i]))
+    copies.append(pltpu.make_async_copy(k_ref, k_hbm, sem.at[pieces]))
+    copies.append(pltpu.make_async_copy(v_ref, v_hbm, sem.at[pieces + 1]))
+    for copy in copies:
+        copy.start()
     for copy in copies:
         copy.wait()
 
@@ -465,8 +472,8 @@
             out_specs=[vmem] * 3 + [hbm],
             out_shape=[
                 pltpu.VMEM((rows, dim), BF16),
-                pltpu.VMEM((rows, cols), BF16),
-                pltpu.VMEM((rows, cols), BF16),
+                pltpu.VMEM((rows, kv_dev, HEAD_DIM), BF16),
+                pltpu.VMEM((rows, kv_dev, HEAD_DIM), BF16),
                 jax.ShapeDtypeStruct(w_o.shape, BF16),
             ],
             scratch_shapes=[
@@ -500,8 +507,8 @@
             in_specs=[vmem] * 3,
             out_specs=[hbm] * 3,
             out_shape=[jax.ShapeDtypeStruct((rows, dim), BF16), cache, cache],
-            scratch_shapes=[pltpu.VMEM(cache.shape, BF16), pltpu.VMEM(cache.shape, BF16), dma((3,))],
-            compiler_params=pltpu.CompilerParams(vmem_limit_bytes=16 * 1024 * 1024),
+            scratch_shapes=[dma((10,))],
+            compiler_params=pltpu.CompilerParams(vmem_limit_bytes=2 * 1024 * 1024),
             name="write",
         )(y_raw, k_flat, v_flat)
 

time: 208 us -> 193 us (0.928)
  Pallas kernels: 207 us -> 192 us
    pallas_call x1, Pallas kernels: 197 us -> 188 us  [device_fn(): pl.pallas_call(layer_kernel, in_specs=[hbm, vmem, vmem, vmem, hbm, hbm, h...]
    pallas_call x1, Pallas kernels: 10 us -> 4.02 us  [device_fn(): pl.pallas_call(write_kernel, in_specs=[vmem] * 3, out_specs=[hbm] * 3, ou...]
where the time goes in v3:
time: 193 us
  Pallas kernels  192 us (99%)
    pallas_call x1, Pallas kernels, device_fn(): pl.pallas_call(layer_kernel, in_specs=[hbm, vmem, vmem, vmem, hbm, hbm, h...  188 us
    pallas_call x1, Pallas kernels, device_fn(): pl.pallas_call(write_kernel, in_specs=[vmem] * 3, out_specs=[hbm] * 3, ou...  4.02 us

profile of v3, /device:TPU:0, one launch (start us, length us, event | category | flops | bytes accessed | tf_op | source)
XLA Modules:
  0.0 192.9 jit_solution(3639869984603627076)
XLA Ops:
  0.6 188.3 %layer.1 = (bf16[1024,4096]{1,0:T(8,128)(2,1)S(1)}, bf16[1024,4,128]{2,1,0:T(4,128)(2,1)S(1)}, bf16[1024,4,128]{2,1,0:T(4,128)(2,1)S(1)}, bf16[2048,4096]{1,0:T(8,128)(2,1)}) custom-call(bf16[1024,4096]{1,0:T(8,128)(2,1)} %x_hbm.1, s32[1,1024]{1,0:T(1,128)} %bitcast.3, f32[64,1]{1,0:T(8,128)} %constant.3.freq_ref, bf16[32,128]{1,0:T(8,128)(2,1)} %bitcast.2, ...), custom_call_target="tpu_custom_call" | custom-call | tf_op jit(solution)/shard_map/layer/pallas_call | solution.py:469
  188.9 4.0 %write.1 = (bf16[1024,4096]{1,0:T(8,128)(2,1)}, bf16[1024,4,128]{2,1,0:T(4,128)(2,1)}, bf16[1024,4,128]{2,1,0:T(4,128)(2,1)}) custom-call(bf16[1024,4096]{1,0:T(8,128)(2,1)S(1)} %get-tuple-element.6.y_ref, bf16[1024,4,128]{2,1,0:T(4,128)(2,1)S(1)} %get-tuple-element.7.k_ref, bf16[1024,4,128]{2,1,0:T(4,128)(2,1)S(1)} %get-tuple-element.8.v_ref), custom_call_target="tpu_custom_call" | custom-call | tf_op jit(solution)/shard_map/write/pallas_call | solution.py:505

commit v4 on v3

--- a/solution.py
+++ b/solution.py
@@ -27,11 +27,11 @@
     return freqs.astype(np.float32)
 
 
-def layer_kernel(x_hbm, pos_ref, freq_ref, gain_ref, wq_hbm, wk_hbm, wv_hbm, wo_hbm,
+def layer_kernel(x_hbm, pos_hbm, freq_hbm, gain_hbm, wq_hbm, wk_hbm, wv_hbm, wo_hbm,
                  y_ref, kst_ref, vst_ref, w1_hbm,
                  hbuf, wbuf, kv_ref, qt_ref, s_even, s_odd, p_even, p_odd,
-                 m_ref, l_ref, att_ref, acc_ref, cos_t, sin_t, gain_f,
-                 x_sem, w_sem, f_sem,
+                 m_ref, l_ref, att_ref, acc_ref, cos_t, sin_t, gain_f, pos_ref, freq_ref, gain_ref,
+                 x_sem, w_sem, f_sem, t_sem,
                  wy_s, wy_r, wx_s, wx_r, wc_s, wc_r, wd_s, wd_r,
                  kc_s, kc_r, kx_s, kx_r, kd_s, kd_r, oy_s, oy_r, or_s, or_r, free_sem):
     rows, dim = hbuf.shape
@@ -85,9 +85,12 @@
     def oy(g):
         return remote(hbuf.at[:, at(g, width)], hbuf.at[:, at(g + n_grp, width)], oy_s.at[g], oy_r.at[g], peer_y)
 
+    tail_rows = (256, 256, 256, 128, 128)
+    tail = [pl.ds(sum(tail_rows[:r]), tail_rows[r]) for r in range(len(tail_rows))]
+
     def o_last(r):
         g = n_grp - 1
-        return remote(hbuf.at[at(r, blk), at(g, width)], hbuf.at[at(r, blk), at(g + n_grp, width)],
+        return remote(hbuf.at[tail[r], at(g, width)], hbuf.at[tail[r], at(g + n_grp, width)],
                       or_s.at[r], or_r.at[r], peer_y)
 
     def x_in(r):
@@ -125,18 +128,23 @@
         for j in range(n_tile):
             w1_in(g, j).start()
 
+    barrier = pltpu.get_barrier_semaphore()
+    for peer in (peer_y, peer_c, peer_x):
+        pl.semaphore_signal(barrier, inc=1, device_id=peer, device_id_type=MESH)
+    tables = [pltpu.make_async_copy(src, dst, t_sem.at[n])
+              for n, (src, dst) in enumerate(((pos_hbm, pos_ref), (freq_hbm, freq_ref), (gain_hbm, gain_ref)))]
+    for copy in tables:
+        copy.start()
     x_in(0).start()
     k_in.start()
     x_in(1).start()
     v_in.start()
     x_in(2).start()
     x_in(3).start()
-    barrier = pltpu.get_barrier_semaphore()
-    for peer in (peer_y, peer_c, peer_x):
-        pl.semaphore_signal(barrier, inc=1, device_id=peer, device_id_type=MESH)
     pl.semaphore_wait(barrier, 3)
     wy(0).start()
-
+    for copy in tables:
+        copy.wait()
     gain = gain_ref[...].astype(F32)
     gain_f[...] = jnp.concatenate([gain[i:i + 1, :] for i in range(gain.shape[0])], axis=1)
 
@@ -410,24 +418,24 @@
     oy(2).wait_recv()
     o_last(2).start()
     load_group(3)
-    add_group(2, lambda: o_last(3).start())
+    add_group(2)
     for j in range(n_tile):
         w1_in(3, j).wait()
 
-    def finish(r, carry):
-        @pl.when(r > 0)
-        def _():
+    for r in range(len(tail)):
+        if r > 0:
             o_last(r).wait_recv()
-
-        rws = at(r, blk)
-        for j in range(n_tile):
-            cols = slice(j * width, (j + 1) * width)
-            total = acc_ref[rws, cols] + jnp.dot(hbuf[rws, at(2 * n_grp - 1, width)], wbuf[1, at(j, width)],
-                                                 preferred_element_type=F32)
-            y_ref[rws, cols] = total.astype(BF16)
-        return carry
-
-    lax.fori_loop(0, n_blk, finish, 0)
+        if 0 < r < len(tail) - 2:
+            o_last(r + 2).start()
+
+        def finish(j, carry):
+            cols = at(j, width)
+            total = acc_ref[tail[r], cols] + jnp.dot(hbuf[tail[r], at(2 * n_grp - 1, width)], wbuf[1, at(j, width)],
+                                                     preferred_element_type=F32)
+            y_ref[tail[r], cols] = total.astype(BF16)
+            return carry
+
+        lax.fori_loop(0, n_tile, finish, 0, unroll=4)
 
     for n in range(4):
         kx(n).wait_send()
@@ -436,9 +444,10 @@
         wx(n).wait_send()
         wc(n).wait_send()
         wd(n).wait_send()
-        o_last(n).wait_send()
     for g in range(3):
         oy(g).wait_send()
+    for r in range(len(tail)):
+        o_last(r).wait_send()
 
 
 def write_kernel(y_ref, k_ref, v_ref, y_hbm, k_hbm, v_hbm, sem):
@@ -468,7 +477,7 @@
         dma = pltpu.SemaphoreType.DMA
         y_raw, k_flat, v_flat, _ = pl.pallas_call(
             layer_kernel,
-            in_specs=[hbm, vmem, vmem, vmem, hbm, hbm, hbm, hbm],
+            in_specs=[hbm] * 8,
             out_specs=[vmem] * 3 + [hbm],
             out_shape=[
                 pltpu.VMEM((rows, dim), BF16),
@@ -492,10 +501,13 @@
                 pltpu.VMEM((half, rows), F32),
                 pltpu.VMEM((half, rows), F32),
                 pltpu.VMEM((1, dim), F32),
-                dma((4,)), dma((4,)), dma((2, 8)),
+                pltpu.VMEM((1, rows), jnp.int32),
+                pltpu.VMEM((half, 1), F32),
+                pltpu.VMEM((dim // HEAD_DIM, HEAD_DIM), BF16),
+                dma((4,)), dma((4,)), dma((2, 8)), dma((3,)),
                 dma((4,)), dma((4,)), dma((4,)), dma((4,)), dma((4,)), dma((4,)), dma((4,)), dma((4,)),
                 dma, dma, dma((4,)), dma((4,)), dma((4,)), dma((4,)),
-                dma((3,)), dma((3,)), dma((4,)), dma((4,)),
+                dma((3,)), dma((3,)), dma((5,)), dma((5,)),
                 pltpu.SemaphoreType.REGULAR,
             ],
             compiler_params=pltpu.CompilerParams(collective_id=0, has_side_effects=True, vmem_limit_bytes=53 * 1024 * 1024),

time: 193 us -> 192 us (level)
  no operation moved by 1% of the time
where the time goes in v4:
time: 192 us
  Pallas kernels  191 us (99%)
    pallas_call x1, Pallas kernels, device_fn(): pl.pallas_call(layer_kernel, in_specs=[hbm] * 8, out_specs=[vmem] * 3 + [...  187 us
    pallas_call x1, Pallas kernels, device_fn(): pl.pallas_call(write_kernel, in_specs=[vmem] * 3, out_specs=[hbm] * 3, ou...  4.02 us

profile of v4, /device:TPU:0, one launch (start us, length us, event | category | flops | bytes accessed | tf_op | source)
XLA Modules:
  0.0 191.9 jit_solution(10059646312051567842)
XLA Ops:
  0.6 187.3 %layer.1 = (bf16[1024,4096]{1,0:T(8,128)(2,1)S(1)}, bf16[1024,4,128]{2,1,0:T(4,128)(2,1)S(1)}, bf16[1024,4,128]{2,1,0:T(4,128)(2,1)S(1)}, bf16[2048,4096]{1,0:T(8,128)(2,1)}) custom-call(bf16[1024,4096]{1,0:T(8,128)(2,1)} %x_hbm.1, s32[1,1024]{1,0:T(1,128)} %bitcast.3, f32[64,1]{1,0:T(8,128)} %constant.3.freq_hbm, bf16[32,128]{1,0:T(8,128)(2,1)} %bitcast.2, ...), custom_call_target="tpu_custom_call" | custom-call | tf_op jit(solution)/shard_map/layer/pallas_call | solution.py:478
  187.9 4.0 %write.1 = (bf16[1024,4096]{1,0:T(8,128)(2,1)}, bf16[1024,4,128]{2,1,0:T(4,128)(2,1)}, bf16[1024,4,128]{2,1,0:T(4,128)(2,1)}) custom-call(bf16[1024,4096]{1,0:T(8,128)(2,1)S(1)} %get-tuple-element.6.y_ref, bf16[1024,4,128]{2,1,0:T(4,128)(2,1)S(1)} %get-tuple-element.7.k_ref, bf16[1024,4,128]{2,1,0:T(4,128)(2,1)S(1)} %get-tuple-element.8.v_ref), custom_call_target="tpu_custom_call" | custom-call | tf_op jit(solution)/shard_map/write/pallas_call | solution.py:517

commit v5 on v4

--- a/solution.py
+++ b/solution.py
@@ -135,14 +135,14 @@
               for n, (src, dst) in enumerate(((pos_hbm, pos_ref), (freq_hbm, freq_ref), (gain_hbm, gain_ref)))]
     for copy in tables:
         copy.start()
+    pl.semaphore_wait(barrier, 3)
+    wy(0).start()
     x_in(0).start()
     k_in.start()
     x_in(1).start()
     v_in.start()
     x_in(2).start()
     x_in(3).start()
-    pl.semaphore_wait(barrier, 3)
-    wy(0).start()
     for copy in tables:
         copy.wait()
     gain = gain_ref[...].astype(F32)
@@ -401,7 +401,8 @@
     oy(1).wait_recv()
     add_group(1)
     pass_on(2)
-    o_last(0).start()
+    for r in range(len(tail)):
+        o_last(r).start()
 
     def caches(c, carry):
         rws = at(c, HEAD_DIM)
@@ -412,21 +413,15 @@
 
     lax.fori_loop(0, rows // HEAD_DIM, caches, 0)
     load_group(2)
-    o_last(0).wait_recv()
-    o_last(1).start()
     pass_on(3)
     oy(2).wait_recv()
-    o_last(2).start()
     load_group(3)
     add_group(2)
     for j in range(n_tile):
         w1_in(3, j).wait()
 
     for r in range(len(tail)):
-        if r > 0:
-            o_last(r).wait_recv()
-        if 0 < r < len(tail) - 2:
-            o_last(r + 2).start()
+        o_last(r).wait_recv()
 
         def finish(j, carry):
             cols = at(j, width)

time: 192 us -> 192 us (level)
  no operation moved by 1% of the time
where the time goes in v5:
time: 192 us
  Pallas kernels  191 us (99%)
    pallas_call x1, Pallas kernels, device_fn(): pl.pallas_call(layer_kernel, in_specs=[hbm] * 8, out_specs=[vmem] * 3 + [...  187 us
    pallas_call x1, Pallas kernels, device_fn(): pl.pallas_call(write_kernel, in_specs=[vmem] * 3, out_specs=[hbm] * 3, ou...  4.02 us

profile of v5, /device:TPU:0, one launch (start us, length us, event | category | flops | bytes accessed | tf_op | source)
XLA Modules:
  0.0 191.5 jit_solution(15642235778150336583)
XLA Ops:
  0.6 186.9 %layer.1 = (bf16[1024,4096]{1,0:T(8,128)(2,1)S(1)}, bf16[1024,4,128]{2,1,0:T(4,128)(2,1)S(1)}, bf16[1024,4,128]{2,1,0:T(4,128)(2,1)S(1)}, bf16[2048,4096]{1,0:T(8,128)(2,1)}) custom-call(bf16[1024,4096]{1,0:T(8,128)(2,1)} %x_hbm.1, s32[1,1024]{1,0:T(1,128)} %bitcast.3, f32[64,1]{1,0:T(8,128)} %constant.3.freq_hbm, bf16[32,128]{1,0:T(8,128)(2,1)} %bitcast.2, ...), custom_call_target="tpu_custom_call" | custom-call | tf_op jit(solution)/shard_map/layer/pallas_call | solution.py:473
  187.5 4.0 %write.1 = (bf16[1024,4096]{1,0:T(8,128)(2,1)}, bf16[1024,4,128]{2,1,0:T(4,128)(2,1)}, bf16[1024,4,128]{2,1,0:T(4,128)(2,1)}) custom-call(bf16[1024,4096]{1,0:T(8,128)(2,1)S(1)} %get-tuple-element.6.y_ref, bf16[1024,4,128]{2,1,0:T(4,128)(2,1)S(1)} %get-tuple-element.7.k_ref, bf16[1024,4,128]{2,1,0:T(4,128)(2,1)S(1)} %get-tuple-element.8.v_ref), custom_call_target="tpu_custom_call" | custom-call | tf_op jit(solution)/shard_map/write/pallas_call | solution.py:512

commit v6 on v5

--- a/solution.py
+++ b/solution.py
@@ -420,6 +420,12 @@
     for j in range(n_tile):
         w1_in(3, j).wait()
 
+    for n in range(4):
+        for copy in (kx, kd, wy, wx, wc, wd):
+            copy(n).wait_send()
+    for g in range(n_grp - 1):
+        oy(g).wait_send()
+
     for r in range(len(tail)):
         o_last(r).wait_recv()
 
@@ -430,17 +436,8 @@
             y_ref[tail[r], cols] = total.astype(BF16)
             return carry
 
-        lax.fori_loop(0, n_tile, finish, 0, unroll=4)
-
-    for n in range(4):
-        kx(n).wait_send()
-        kd(n).wait_send()
-        wy(n).wait_send()
-        wx(n).wait_send()
-        wc(n).wait_send()
-        wd(n).wait_send()
-    for g in range(3):
-        oy(g).wait_send()
+        lax.fori_loop(0, n_tile, finish, 0, unroll=True)
+
     for r in range(len(tail)):
         o_last(r).wait_send()
 

time: 192 us -> 192 us (level)
  no operation moved by 1% of the time
where the time goes in v6:
time: 192 us; the launch traced here: 191 us
  Pallas kernels  191 us (99%)
    pallas_call x1, Pallas kernels, device_fn(): pl.pallas_call(layer_kernel, in_specs=[hbm] * 8, out_specs=[vmem] * 3 + [...  187 us
    pallas_call x1, Pallas kernels, device_fn(): pl.pallas_call(write_kernel, in_specs=[vmem] * 3, out_specs=[hbm] * 3, ou...  4.02 us

profile of v6, /device:TPU:0, one launch (start us, length us, event | category | flops | bytes accessed | tf_op | source)
XLA Modules:
  0.0 191.4 jit_solution(425520157956039015)
XLA Ops:
  0.6 186.6 %layer.1 = (bf16[1024,4096]{1,0:T(8,128)(2,1)S(1)}, bf16[1024,4,128]{2,1,0:T(4,128)(2,1)S(1)}, bf16[1024,4,128]{2,1,0:T(4,128)(2,1)S(1)}, bf16[2048,4096]{1,0:T(8,128)(2,1)}) custom-call(bf16[1024,4096]{1,0:T(8,128)(2,1)} %x_hbm.1, s32[1,1024]{1,0:T(1,128)} %bitcast.3, f32[64,1]{1,0:T(8,128)} %constant.3.freq_hbm, bf16[32,128]{1,0:T(8,128)(2,1)} %bitcast.2, ...), custom_call_target="tpu_custom_call" | custom-call | tf_op jit(solution)/shard_map/layer/pallas_call | solution.py:470
  187.3 4.0 %write.1 = (bf16[1024,4096]{1,0:T(8,128)(2,1)}, bf16[1024,4,128]{2,1,0:T(4,128)(2,1)}, bf16[1024,4,128]{2,1,0:T(4,128)(2,1)}) custom-call(bf16[1024,4096]{1,0:T(8,128)(2,1)S(1)} %get-tuple-element.6.y_ref, bf16[1024,4,128]{2,1,0:T(4,128)(2,1)S(1)} %get-tuple-element.7.k_ref, bf16[1024,4,128]{2,1,0:T(4,128)(2,1)S(1)} %get-tuple-element.8.v_ref), custom_call_target="tpu_custom_call" | custom-call | tf_op jit(solution)/shard_map/write/pallas_call | solution.py:509
